TPU v7x, 32 devices: a whole 2x2x4 slice. The times are simulated.
32 devices in a mesh: expert: 4 (over z), shard: 8 (over y, x, core).
Axes of the slice: x: 2, y: 2, z: 4, core: 2. Of those that a mesh axis runs over, the one named last changes fastest.
Arguments:
- master_gate: float32 [64, 2048, 1408], P('expert', 'shard'), may hold values from -0.1875 to 0.1875
- master_up: float32 [64, 2048, 1408], P('expert', 'shard'), may hold values from -0.1875 to 0.1875
- router_weight: float32 [2048, 64], P('shard', 'expert'), may hold values from -0.125 to 0.125
- router_gain: float32 [2048], P('shard'), may hold values from 0.25 to 1.75
Outputs:
- final_gate: bfloat16 [64, 2048, 1408], P('expert', None, 'shard')
- final_up: bfloat16 [64, 2048, 1408], P('expert', None, 'shard')
- scale_gate: float32 [64, 1408], P('expert', 'shard')
- scale_up: float32 [64, 1408], P('expert', 'shard')
- serve_router: bfloat16 [2048, 64], replicated
All inputs are finite; a program needn't handle non-finite values.
Results may differ from a plain program's by a relative error of at most 0.001.
Values may be sent and summed in bfloat16 or wider, within the bound.
A program may use at most 192 MiB of HBM per device.

v0:
```python
import jax
import jax.numpy as jnp
from jax import lax
from jax.sharding import PartitionSpec as P


def local(master_gate, master_up, router_weight, router_gain):
    total_gate, total_up = lax.psum(
        (jnp.sum(master_gate * master_gate, axis=1), jnp.sum(master_up * master_up, axis=1)),
        "shard",
    )
    scale_gate = jnp.sqrt(total_gate)
    scale_up = jnp.sqrt(total_up)
    narrow_gate, narrow_up = (
        (master_gate / jnp.expand_dims(scale_gate, 1)).astype(jnp.bfloat16),
        (master_up / jnp.expand_dims(scale_up, 1)).astype(jnp.bfloat16),
    )
    final_gate, final_up = (
        lax.all_to_all(narrow_gate, "shard", split_axis=2, concat_axis=1, tiled=True),
        lax.all_to_all(narrow_up, "shard", split_axis=2, concat_axis=1, tiled=True),
    )
    scale_gate = lax.dynamic_slice_in_dim(
        scale_gate, lax.axis_index("shard") * final_gate.shape[2], final_gate.shape[2], axis=1
    )
    scale_up = lax.dynamic_slice_in_dim(
        scale_up, lax.axis_index("shard") * final_up.shape[2], final_up.shape[2], axis=1
    )
    part_router = (router_weight * router_gain[:, None]).astype(jnp.bfloat16)
    row_router = lax.all_gather(part_router, "shard", axis=0, tiled=True)
    serve_router = lax.all_gather(row_router, "expert", axis=1, tiled=True)
    return (final_gate, final_up, scale_gate, scale_up, serve_router)


def solution(mesh):
    in_specs = (
        P("expert", "shard", None),
        P("expert", "shard", None),
        P("shard", "expert"),
        P("shard"),
    )
    out_specs = (
        P("expert", None, "shard"),
        P("expert", None, "shard"),
        P("expert", "shard"),
        P("expert", "shard"),
        P(),
    )
    return jax.shard_map(local, mesh=mesh, in_specs=in_specs, out_specs=out_specs, check_vma=False)
```

profile of v0, /device:TPU:0, one launch (start us, length us, event | category | flops | bytes accessed | tf_op | source)
XLA Modules:
  0.0 445.2 jit_solution(13781813590717320649)
XLA Ops:
  7.2 0.0 all-reduce.3.cloned.1.call-start
  7.2 15.8 %multiply_reduce_fusion = (f32[16,1408]{1,0:T(8,128)}, f32[16,1408]{1,0:T(8,128)}) fusion(f32[16,256,1408]{2,1,0:T(8,128)} %param.5, f32[16,256,1408]{2,1,0:T(8,128)} %param.4), kind=kLoop, calls=%fused_computation.1 | loop fusion | flops 23023616 | bytes 46317568 | tf_op jit(solution)/shard_map/reduce_sum | solution.py:9
  23.0 0.0 all-reduce.3.cloned.1.call-update
  23.1 23.7 %copy.22 = f32[16,256,1408]{1,0,2:T(8,128)} copy(f32[16,256,1408]{2,1,0:T(8,128)} %param.5) | data formatting | bytes 46137344 | tf_op args[1]
  46.8 32.3 %all-reduce.3.cloned.1.call-done = (f32[16,1408]{1,0:T(8,128)}, f32[16,1408]{1,0:T(8,128)}) async-done(((f32[16,1408]{1,0:T(8,128)}, f32[16,1408]{1,0:T(8,128)}), (f32[16,1408]{1,0:T(8,128)}, f32[16,1408]{1,0:T(8,128)})) %all-reduce.3.cloned.1.call-update) | async-done | bytes 180240 | tf_op jit(solution)/shard_map/psum | solution.py:8
  79.0 0.9 sqrt.7
  80.0 0.3 copy.21
  80.2 14.2 %divide_convert_fusion = bf16[16,256,1408]{1,0,2:T(8,128)(2,1)} fusion(f32[16,256,1408]{1,0,2:T(8,128)} %copy.22, f32[16,1408]{0,1:T(8,128)S(1)} %copy.21), kind=kLoop, calls=%fused_computation | loop fusion | flops 11534336 | bytes 34693120 | tf_op jit(solution)/shard_map/convert_element_type | solution.py:16
  94.4 5.2 %all-to-all-start.1 = ((bf16[16,256,1408]{1,0,2:T(8,128)(2,1)}), bf16[16,256,1408]{1,0,2:T(8,128)(2,1)}, u32[]{:S(2)}, u32[]{:S(2)}) async-start(bf16[16,256,1408]{1,0,2:T(8,128)(2,1)} %divide_convert_fusion), calls=%async_computation.1 | async-start | bytes 23068672 | tf_op jit(solution)/shard_map/all_to_all | solution.py:20
  99.7 0.0 copy-start
  99.7 23.7 %copy.18 = f32[16,256,1408]{1,0,2:T(8,128)} copy(f32[16,256,1408]{2,1,0:T(8,128)} %param.4) | data formatting | bytes 46137344 | tf_op args[0]
  123.4 0.0 copy-done
  123.4 0.3 copy.17
  123.7 0.0 copy-start.1
  123.7 0.0 copy-start.2
  123.7 14.2 %divide_convert_fusion.1 = bf16[16,256,1408]{1,0,2:T(8,128)(2,1)} fusion(f32[16,256,1408]{1,0,2:T(8,128)} %copy.18, f32[16,1408]{0,1:T(8,128)S(1)} %copy.17), kind=kLoop, calls=%fused_computation.2 | loop fusion | flops 11534336 | bytes 34693120 | tf_op jit(solution)/shard_map/convert_element_type | solution.py:15
  138.0 89.5 %all-to-all-done.1 = bf16[16,256,1408]{1,0,2:T(8,128)(2,1)} async-done(((bf16[16,256,1408]{1,0,2:T(8,128)(2,1)}), bf16[16,256,1408]{1,0,2:T(8,128)(2,1)}, u32[]{:S(2)}, u32[]{:S(2)}) %all-to-all-start.1) | async-done | bytes 11534368 | tf_op jit(solution)/shard_map/all_to_all | solution.py:20
  227.4 5.3 %all-to-all-start = ((bf16[16,256,1408]{1,0,2:T(8,128)(2,1)}), bf16[16,256,1408]{1,0,2:T(8,128)(2,1)}, u32[]{:S(2)}, u32[]{:S(2)}) async-start(bf16[16,256,1408]{1,0,2:T(8,128)(2,1)} %divide_convert_fusion.1), calls=%async_computation | async-start | bytes 23068672 | tf_op jit(solution)/shard_map/all_to_all | solution.py:19
  232.7 0.0 copy-done.1
  232.7 0.0 copy-done.2
  232.7 130.9 %all_gather.6 = bf16[2048,16]{0,1:T(8,128)(2,1)S(1)} all-gather(bf16[256,16]{0,1:T(8,128)(2,1)S(1)} %multiply_convert_fusion), channel_id=1, replica_groups=mesh['expert'=4,'shard'=8] {'shard'}, dimensions={0}, use_global_device_ids=true | all-gather | bytes 73728 | tf_op jit(solution)/shard_map/all_gather | solution.py:29
  363.6 14.0 %all_gather.7 = bf16[2048,64]{0,1:T(8,128)(2,1)S(1)} all-gather(bf16[2048,16]{0,1:T(8,128)(2,1)S(1)} %all_gather.6), channel_id=1, replica_groups=mesh['expert'=4,'shard'=8] {'expert'}, dimensions={1}, use_global_device_ids=true | all-gather | bytes 327680 | tf_op jit(solution)/shard_map/all_gather | solution.py:30
  377.6 0.7 constant_dynamic-slice_fusion
  378.3 0.7 constant_dynamic-slice_fusion.1
  379.0 11.4 %copy.24 = bf16[16,8,256,176]{2,1,3,0:T(8,128)(2,1)} copy(bf16[16,8,256,176]{2,0,3,1:T(8,128)(2,1)} %bitcast.5) | data formatting | bytes 23068672 | tf_op jit(solution)/shard_map/all_to_all | solution.py:20
  390.4 18.0 %all_to_all.33 = bf16[16,2048,176]{1,2,0:T(8,128)(2,1)} reshape(bf16[16,8,256,176]{2,1,3,0:T(8,128)(2,1)} %copy.24) | data formatting | bytes 23068672 | tf_op jit(solution)/shard_map/all_to_all | solution.py:20
  408.3 0.0 all-to-all-done
  408.3 11.4 %copy.20 = bf16[16,8,256,176]{2,1,3,0:T(8,128)(2,1)} copy(bf16[16,8,256,176]{2,0,3,1:T(8,128)(2,1)} %bitcast.2) | data formatting | bytes 23068672 | tf_op jit(solution)/shard_map/all_to_all | solution.py:19
  419.7 18.0 %all_to_all.29 = bf16[16,2048,176]{1,2,0:T(8,128)(2,1)} reshape(bf16[16,8,256,176]{2,1,3,0:T(8,128)(2,1)} %copy.20) | data formatting | bytes 23068672 | tf_op jit(solution)/shard_map/all_to_all | solution.py:19
  437.7 0.7 copy.30
  (2 shorter events, 0.0 us)
Async XLA Ops:
  7.2 71.9 %all-reduce.3.cloned.1.call-start = ((), (), s32[]{:S(2)}) async-start(), calls=%async_computation.2 | async-start | bytes 360448 | tf_op jit(solution)/shard_map/psum | solution.py:8
  94.4 133.0 %all-to-all-start.1 = ((bf16[16,256,1408]{1,0,2:T(8,128)(2,1)}), bf16[16,256,1408]{1,0,2:T(8,128)(2,1)}, u32[]{:S(2)}, u32[]{:S(2)}) async-start(bf16[16,256,1408]{1,0,2:T(8,128)(2,1)} %divide_convert_fusion), calls=%async_computation.1 | async-start | bytes 23068672 | tf_op jit(solution)/shard_map/all_to_all | solution.py:20
  99.7 23.7 %copy-start = (f32[16,1408]{1,0:T(8,128)S(1)}, f32[16,1408]{1,0:T(8,128)}, u32[]{:S(2)}) copy-start(f32[16,1408]{1,0:T(8,128)} %get-tuple-element.5) | copy-start | bytes 270340
  123.7 109.0 %copy-start.1 = (f32[256,16]{0,1:T(8,128)S(1)}, f32[256,16]{0,1:T(8,128)}, u32[]{:S(2)}) copy-start(f32[256,16]{0,1:T(8,128)} %param.6) | copy-start | bytes 49156
  123.7 109.0 %copy-start.2 = (f32[256]{0:T(256)S(1)}, f32[256]{0:T(256)}, u32[]{:S(2)}) copy-start(f32[256]{0:T(256)} %param.7) | copy-start | bytes 3076
  227.4 180.9 %all-to-all-start = ((bf16[16,256,1408]{1,0,2:T(8,128)(2,1)}), bf16[16,256,1408]{1,0,2:T(8,128)(2,1)}, u32[]{:S(2)}, u32[]{:S(2)}) async-start(bf16[16,256,1408]{1,0,2:T(8,128)(2,1)} %divide_convert_fusion.1), calls=%async_computation | async-start | bytes 23068672 | tf_op jit(solution)/shard_map/all_to_all | solution.py:19
Sparse Core Ops, SparseCore 0:
  23.2 55.8 all-reduce.2
where the time goes:
time: 447 us; the launch traced here: 445 us
  blocking collectives  145 us (32%)
  waiting for transfers between devices  122 us (27%)
  local copies, waits for them, and re-layouts  110 us (25%)
  other arithmetic  44.3 us (10%)
  between operations  14.1 us (3%)
  starting transfers between devices  10.5 us (2%)
    all_gather x1, blocking collectives, local(): row_router = lax.all_gather(part_router, 'shard', axis=0, tiled=True)  131 us
    all_to_all x1, waiting for transfers between devices, local(): lax.all_to_all(narrow_up, 'shard', split_axis=2, concat_axis=1, tiled=True)  89.5 us
    unnamed x9, local copies, waits for them, and re-layouts  48.1 us
    psum x1, waiting for transfers between devices, local(): lax.psum((jnp.sum(master_gate * master_gate, axis=1), jnp.sum(master_up *...  32.3 us
    all_to_all x2, local copies, waits for them, and re-layouts, local(): lax.all_to_all(narrow_gate, 'shard', split_axis=2, concat_axis=1, tiled=T...  29.3 us
    all_to_all x2, local copies, waits for them, and re-layouts, local(): lax.all_to_all(narrow_up, 'shard', split_axis=2, concat_axis=1, tiled=True)  29.3 us
    reduce_sum x1, other arithmetic, local(): jnp.sum(master_up * master_up, axis=1)  15.8 us
    convert_element_type x1, other arithmetic, local(): (master_up / jnp.expand_dims(scale_up, 1)).astype(jnp.bfloat16)  14.2 us
  transfers between devices with their start and end apart: 3, of which 2 were waited for; matrix products, arithmetic and copies ran while one was open for 17% of the time, Pallas kernels for 0%

commit v1 on v0

--- a/solution.py
+++ b/solution.py
@@ -26,7 +26,14 @@
         scale_up, lax.axis_index("shard") * final_up.shape[2], final_up.shape[2], axis=1
     )
     part_router = (router_weight * router_gain[:, None]).astype(jnp.bfloat16)
-    row_router = lax.all_gather(part_router, "shard", axis=0, tiled=True)
+    ring = [part_router]
+    for hop in range(7):
+        ring.append(lax.ppermute(ring[-1], "shard", [(dev, (dev + 1) % 8) for dev in range(8)]))
+    row_router = jnp.roll(
+        jnp.concatenate(ring[::-1], axis=0),
+        (lax.axis_index("shard") + 1) * ring[0].shape[0],
+        axis=0,
+    )
     serve_router = lax.all_gather(row_router, "expert", axis=1, tiled=True)
     return (final_gate, final_up, scale_gate, scale_up, serve_router)
 

time: 447 us -> 468 us (1.047)
  waiting for transfers between devices: 122 us -> 272 us
  blocking collectives: 145 us -> 14.4 us
    ppermute x0 -> x7, waiting for transfers between devices: none -> 151 us  [local(): lax.ppermute(ring[-1], 'shard', [(dev, (dev + 1) % 8) for dev in range(8)])]
    all_gather x1 -> x0, blocking collectives: 131 us -> none  [local(): row_router = lax.all_gather(part_router, 'shard', axis=0, tiled=True)]
    all_to_all x1, waiting for transfers between devices: 89.5 us -> 0.01 us  [local(): lax.all_to_all(narrow_up, 'shard', split_axis=2, concat_axis=1, tiled=True)]
    all_to_all x1, waiting for transfers between devices: 0.01 us -> 89.5 us  [local(): lax.all_to_all(narrow_gate, 'shard', split_axis=2, concat_axis=1, tiled=T...]
    unnamed x9 -> x23, local copies, waits for them, and re-layouts: 48.1 us -> 48.1 us
  transfers between devices with their start and end apart: 3 -> 10, of which waited for: 2 -> 9; matrix products, arithmetic and copies ran while one was open for 17% -> 16% of each run, Pallas kernels for 0% -> 0%
where the time goes in v1:
time: 468 us; the launch traced here: 466 us
  waiting for transfers between devices  272 us (58%)
  local copies, waits for them, and re-layouts  110 us (24%)
  other arithmetic  44.3 us (9%)
  blocking collectives  14.4 us (3%)
  between operations  14.2 us (3%)
  starting transfers between devices  11 us (2%)
    ppermute x7, waiting for transfers between devices, local(): lax.ppermute(ring[-1], 'shard', [(dev, (dev + 1) % 8) for dev in range(8)])  151 us
    all_to_all x1, waiting for transfers between devices, local(): lax.all_to_all(narrow_gate, 'shard', split_axis=2, concat_axis=1, tiled=T...  89.5 us
    unnamed x23, local copies, waits for them, and re-layouts  48.1 us
    psum x1, waiting for transfers between devices, local(): lax.psum((jnp.sum(master_gate * master_gate, axis=1), jnp.sum(master_up *...  32.3 us
    all_to_all x2, local copies, waits for them, and re-layouts, local(): lax.all_to_all(narrow_up, 'shard', split_axis=2, concat_axis=1, tiled=True)  29.3 us
    all_to_all x2, local copies, waits for them, and re-layouts, local(): lax.all_to_all(narrow_gate, 'shard', split_axis=2, concat_axis=1, tiled=T...  29.3 us
    reduce_sum x1, other arithmetic, local(): jnp.sum(master_up * master_up, axis=1)  15.8 us
    all_gather x1, blocking collectives, local(): serve_router = lax.all_gather(row_router, 'expert', axis=1, tiled=True)  14.4 us
  transfers between devices with their start and end apart: 10, of which 9 were waited for; matrix products, arithmetic and copies ran while one was open for 16% of the time, Pallas kernels for 0%

profile of v1, /device:TPU:0, one launch (start us, length us, event | category | flops | bytes accessed | tf_op | source)
XLA Modules:
  0.0 465.9 jit_solution(12689539021334637205)
XLA Ops:
  7.2 0.0 all-reduce.3.cloned.1.call-start
  7.2 15.8 %multiply_reduce_fusion = (f32[16,1408]{1,0:T(8,128)}, f32[16,1408]{1,0:T(8,128)}) fusion(f32[16,256,1408]{2,1,0:T(8,128)} %param.5, f32[16,256,1408]{2,1,0:T(8,128)} %param.4), kind=kLoop, calls=%fused_computation.1 | loop fusion | flops 23023616 | bytes 46317568 | tf_op jit(solution)/shard_map/reduce_sum | solution.py:9
  23.0 0.0 all-reduce.3.cloned.1.call-update
  23.1 23.7 %copy.18 = f32[16,256,1408]{1,0,2:T(8,128)} copy(f32[16,256,1408]{2,1,0:T(8,128)} %param.4) | data formatting | bytes 46137344 | tf_op args[0]
  46.8 32.3 %all-reduce.3.cloned.1.call-done = (f32[16,1408]{1,0:T(8,128)}, f32[16,1408]{1,0:T(8,128)}) async-done(((f32[16,1408]{1,0:T(8,128)}, f32[16,1408]{1,0:T(8,128)}), (f32[16,1408]{1,0:T(8,128)}, f32[16,1408]{1,0:T(8,128)})) %all-reduce.3.cloned.1.call-update) | async-done | bytes 180240 | tf_op jit(solution)/shard_map/psum | solution.py:8
  79.0 0.9 sqrt.6
  80.0 0.3 copy.17
  80.2 14.2 %divide_convert_fusion.1 = bf16[16,256,1408]{1,0,2:T(8,128)(2,1)} fusion(f32[16,256,1408]{1,0,2:T(8,128)} %copy.18, f32[16,1408]{0,1:T(8,128)S(1)} %copy.17), kind=kLoop, calls=%fused_computation.2 | loop fusion | flops 11534336 | bytes 34693120 | tf_op jit(solution)/shard_map/convert_element_type | solution.py:15
  94.4 5.2 %all-to-all-start = ((bf16[16,256,1408]{1,0,2:T(8,128)(2,1)}), bf16[16,256,1408]{1,0,2:T(8,128)(2,1)}, u32[]{:S(2)}, u32[]{:S(2)}) async-start(bf16[16,256,1408]{1,0,2:T(8,128)(2,1)} %divide_convert_fusion.1), calls=%async_computation | async-start | bytes 23068672 | tf_op jit(solution)/shard_map/all_to_all | solution.py:19
  99.7 0.0 copy-start.1
  99.7 23.7 %copy.22 = f32[16,256,1408]{1,0,2:T(8,128)} copy(f32[16,256,1408]{2,1,0:T(8,128)} %param.5) | data formatting | bytes 46137344 | tf_op args[1]
  123.4 0.0 copy-done.1
  123.4 0.3 copy.21
  123.7 0.0 copy-start
  123.7 0.0 copy-start.2
  123.7 14.2 %divide_convert_fusion = bf16[16,256,1408]{1,0,2:T(8,128)(2,1)} fusion(f32[16,256,1408]{1,0,2:T(8,128)} %copy.22, f32[16,1408]{0,1:T(8,128)S(1)} %copy.21), kind=kLoop, calls=%fused_computation | loop fusion | flops 11534336 | bytes 34693120 | tf_op jit(solution)/shard_map/convert_element_type | solution.py:16
  138.0 89.5 %all-to-all-done = bf16[16,256,1408]{1,0,2:T(8,128)(2,1)} async-done(((bf16[16,256,1408]{1,0,2:T(8,128)(2,1)}), bf16[16,256,1408]{1,0,2:T(8,128)(2,1)}, u32[]{:S(2)}, u32[]{:S(2)}) %all-to-all-start) | async-done | bytes 11534368 | tf_op jit(solution)/shard_map/all_to_all | solution.py:19
  227.4 5.3 %all-to-all-start.1 = ((bf16[16,256,1408]{1,0,2:T(8,128)(2,1)}), bf16[16,256,1408]{1,0,2:T(8,128)(2,1)}, u32[]{:S(2)}, u32[]{:S(2)}) async-start(bf16[16,256,1408]{1,0,2:T(8,128)(2,1)} %divide_convert_fusion), calls=%async_computation.1 | async-start | bytes 23068672 | tf_op jit(solution)/shard_map/all_to_all | solution.py:20
  232.7 0.0 copy-done
  232.7 0.0 copy-done.2
  232.7 0.4 collective-permute-start
  233.2 126.8 %collective-permute-done = bf16[256,16]{0,1:T(8,128)(2,1)S(1)} collective-permute-done((bf16[256,16]{0,1:T(8,128)(2,1)S(1)}, bf16[256,16]{0,1:T(8,128)(2,1)S(1)}, u32[]{:S(2)}, u32[]{:S(2)}) %collective-permute-start) | collective-permute-done | bytes 8224 | tf_op jit(solution)/shard_map/ppermute | solution.py:31
  360.0 0.0 collective-permute-start.1
  360.0 4.0 collective-permute-done.1
  363.9 0.0 collective-permute-start.2
  363.9 4.0 collective-permute-done.2
  367.9 0.0 collective-permute-start.3
  367.9 4.0 collective-permute-done.3
  371.9 0.0 collective-permute-start.4
  371.9 4.0 collective-permute-done.4
  375.9 0.0 collective-permute-start.5
  375.9 4.0 collective-permute-done.5
  379.8 0.0 collective-permute-start.6
  379.8 4.0 collective-permute-done.6
  384.0 14.4 %all_gather.3 = bf16[2048,64]{0,1:T(8,128)(2,1)S(1)} all-gather(bf16[2048,16]{0,1:T(8,128)(2,1)S(1)} %constant_dynamic-slice_fusion), channel_id=1, replica_groups=mesh['expert'=4,'shard'=8] {'expert'}, dimensions={1}, use_global_device_ids=true | all-gather | bytes 327680 | tf_op jit(solution)/shard_map/all_gather | solution.py:37
  398.4 0.7 constant_dynamic-slice_fusion.2
  399.1 0.7 constant_dynamic-slice_fusion.1
  399.7 11.3 %copy.20 = bf16[16,8,256,176]{2,1,3,0:T(8,128)(2,1)} copy(bf16[16,8,256,176]{2,0,3,1:T(8,128)(2,1)} %bitcast.2) | data formatting | bytes 23068672 | tf_op jit(solution)/shard_map/all_to_all | solution.py:19
  411.1 18.0 %all_to_all.29 = bf16[16,2048,176]{1,2,0:T(8,128)(2,1)} reshape(bf16[16,8,256,176]{2,1,3,0:T(8,128)(2,1)} %copy.20) | data formatting | bytes 23068672 | tf_op jit(solution)/shard_map/all_to_all | solution.py:19
  429.0 0.0 all-to-all-done.1
  429.0 11.4 %copy.24 = bf16[16,8,256,176]{2,1,3,0:T(8,128)(2,1)} copy(bf16[16,8,256,176]{2,0,3,1:T(8,128)(2,1)} %bitcast.5) | data formatting | bytes 23068672 | tf_op jit(solution)/shard_map/all_to_all | solution.py:20
  440.4 18.0 %all_to_all.33 = bf16[16,2048,176]{1,2,0:T(8,128)(2,1)} reshape(bf16[16,8,256,176]{2,1,3,0:T(8,128)(2,1)} %copy.24) | data formatting | bytes 23068672 | tf_op jit(solution)/shard_map/all_to_all | solution.py:20
  458.4 0.7 copy.45
  (19 shorter events, 0.1 us)
Async XLA Ops:
  7.2 71.9 %all-reduce.3.cloned.1.call-start = ((), (), s32[]{:S(2)}) async-start(), calls=%async_computation.2 | async-start | bytes 360448 | tf_op jit(solution)/shard_map/psum | solution.py:8
  94.4 133.0 %all-to-all-start = ((bf16[16,256,1408]{1,0,2:T(8,128)(2,1)}), bf16[16,256,1408]{1,0,2:T(8,128)(2,1)}, u32[]{:S(2)}, u32[]{:S(2)}) async-start(bf16[16,256,1408]{1,0,2:T(8,128)(2,1)} %divide_convert_fusion.1), calls=%async_computation | async-start | bytes 23068672 | tf_op jit(solution)/shard_map/all_to_all | solution.py:19
  99.7 23.7 %copy-start.1 = (f32[16,1408]{1,0:T(8,128)S(1)}, f32[16,1408]{1,0:T(8,128)}, u32[]{:S(2)}) copy-start(f32[16,1408]{1,0:T(8,128)} %get-tuple-element.6) | copy-start | bytes 270340
  123.7 109.0 %copy-start = (f32[256,16]{0,1:T(8,128)S(1)}, f32[256,16]{0,1:T(8,128)}, u32[]{:S(2)}) copy-start(f32[256,16]{0,1:T(8,128)} %param.6) | copy-start | bytes 49156
  123.7 109.0 %copy-start.2 = (f32[256]{0:T(256)S(1)}, f32[256]{0:T(256)}, u32[]{:S(2)}) copy-start(f32[256]{0:T(256)} %param.7) | copy-start | bytes 3076
  227.4 201.6 %all-to-all-start.1 = ((bf16[16,256,1408]{1,0,2:T(8,128)(2,1)}), bf16[16,256,1408]{1,0,2:T(8,128)(2,1)}, u32[]{:S(2)}, u32[]{:S(2)}) async-start(bf16[16,256,1408]{1,0,2:T(8,128)(2,1)} %divide_convert_fusion), calls=%async_computation.1 | async-start | bytes 23068672 | tf_op jit(solution)/shard_map/all_to_all | solution.py:20
  232.7 127.2 %collective-permute-start = (bf16[256,16]{0,1:T(8,128)(2,1)S(1)}, bf16[256,16]{0,1:T(8,128)(2,1)S(1)}, u32[]{:S(2)}, u32[]{:S(2)}) collective-permute-start(bf16[256,16]{0,1:T(8,128)(2,1)S(1)} %multiply_convert_fusion), channel_id=1, source_target_pairs={{0,1},{1,2},{2,3},{3,4},{4,5},{5,6},{6,7},{7,0},{8,9},{9,10},{10,1... | collective-permute-start | bytes 24584 | tf_op jit(solution)/shard_map/ppermute | solution.py:31
  360.0 4.0 collective-permute-start.1
  363.9 4.0 collective-permute-start.2
  367.9 4.0 collective-permute-start.3
  371.9 4.0 collective-permute-start.4
  375.9 4.0 collective-permute-start.5
  379.8 4.0 collective-permute-start.6
Sparse Core Ops, SparseCore 0:
  23.2 55.8 all-reduce.2
